TPU v7x, 32 devices: a whole 2x2x4 slice. The times are simulated.
32 devices in a mesh: farcp: 4 (over z), nearcp: 4 (over y, x), tp: 2 (over core).
Axes of the slice: x: 2, y: 2, z: 4, core: 2. Of those that a mesh axis runs over, the one named last changes fastest.
Arguments:
- raw_keys: bfloat16 [16, 8192, 8, 128], P(None, ('farcp', 'nearcp'), 'tp'), may hold values from -6 to 6
- raw_values: bfloat16 [16, 8192, 8, 128], P(None, ('farcp', 'nearcp'), 'tp'), may hold values from -6 to 6
- turn_angle: float32 [8192, 64], replicated, may hold values from -3.140625 to 3.140625
Outputs:
- stored_keys: bfloat16 [16, 8192, 8, 128], P(('farcp', 'nearcp'), None, 'tp')
- stored_values: bfloat16 [16, 8192, 8, 128], P(('farcp', 'nearcp'), None, 'tp')
- key_scale: float32 [16, 8, 128], P(('farcp', 'nearcp'), 'tp')
All inputs are finite; a program needn't handle non-finite values. Where the computation divides by a largest or mean magnitude, that divisor is 1e-20 or more.
Results may differ from a plain program's by a relative error of at most 0.001.
Values may be sent and summed in bfloat16 or wider, within the bound.
No kernel may reach another device: no remote copies, remote signals or barrier semaphores. Data moves between devices by JAX's collectives and lax.ppermute only.
A program may use at most 128 MiB of HBM per device.

v0:
```python
import jax
import jax.numpy as jnp
from jax import lax
from jax.sharding import PartitionSpec as P


def turn_pairs(vectors, angle):
    half = vectors.shape[-1] // 2
    cosine, sine = (jnp.cos(angle)[None, :, None, :], jnp.sin(angle)[None, :, None, :])
    first, second = (vectors[..., :half], vectors[..., half:])
    return jnp.concatenate(
        [first * cosine - second * sine, second * cosine + first * sine], axis=-1
    )


def ready_to_store(plain_keys, angle):
    wide_keys = plain_keys.astype(jnp.float32)
    return turn_pairs(wide_keys, angle)


def body(raw_keys, raw_values, turn_angle):
    moved_keys, stored_values = (
        lax.all_to_all(raw_keys, ("farcp", "nearcp"), split_axis=0, concat_axis=1, tiled=True),
        lax.all_to_all(raw_values, ("farcp", "nearcp"), split_axis=0, concat_axis=1, tiled=True),
    )
    turned_keys = ready_to_store(moved_keys, turn_angle)
    key_scale = jnp.max(jnp.abs(turned_keys), axis=1)
    narrow_keys = (turned_keys / key_scale[:, None]).astype(jnp.bfloat16)
    return (narrow_keys, stored_values, key_scale)


def solution(mesh):
    placed = (
        P(None, ("farcp", "nearcp"), "tp", None),
        P(None, ("farcp", "nearcp"), "tp", None),
        P(),
    )
    return jax.shard_map(
        body,
        mesh=mesh,
        in_specs=placed,
        out_specs=(
            P(("farcp", "nearcp"), None, "tp", None),
            P(("farcp", "nearcp"), None, "tp", None),
            P(("farcp", "nearcp"), "tp", None),
        ),
        check_vma=False,
    )
```

profile of v0, /device:TPU:28, one launch (start us, length us, event | category | flops | bytes accessed | tf_op | source)
XLA Modules:
  0.0 390.4 jit_solution(15981875329838903006)
XLA Ops:
  0.6 188.6 %all_to_all.21 = bf16[16,512,4,128]{3,2,1,0:T(4,128)(2,1)} all-to-all(bf16[16,512,4,128]{3,2,1,0:T(4,128)(2,1)} %param.3), channel_id=1, replica_groups=mesh['farcp'=4,'nearcp'=4,'tp'=2] {'farcp','nearcp'}, dimensions={0} | all-to-all | bytes 16777216 | tf_op jit(solution)/shard_map/all_to_all | solution.py:23
  189.2 6.7 %all-to-all-start.1 = ((bf16[16,512,4,128]{3,2,1,0:T(4,128)(2,1)}), bf16[16,512,4,128]{3,2,1,0:T(4,128)(2,1)}, u32[]{:S(2)}, u32[]{:S(2)}) async-start(bf16[16,512,4,128]{3,2,1,0:T(4,128)(2,1)} %param.4), calls=%async_computation.1 | async-start | bytes 16777216 | tf_op jit(solution)/shard_map/all_to_all | solution.py:24
  196.0 9.4 %fusion = (f32[8192,64]{0,1:T(8,128)}, f32[8192,64]{0,1:T(8,128)S(1)}) fusion(f32[8192,64]{0,1:T(8,128)} %param.5), kind=kLoop, calls=%fused_computation.6 | loop fusion | bytes 6291456 | tf_op jit(solution)/shard_map/cos | solution.py:9
  205.4 3.8 copy.6
  209.2 2.8 copy.7
  212.0 0.0 copy-start.2
  212.0 0.0 copy-start.3
  212.0 5.9 %bitcast_convert_fusion = f32[1,4096,8,128]{3,2,1,0:T(8,128)S(1)} fusion(bf16[1,4096,8,128]{3,2,1,0:T(8,128)(2,1)} %bitcast.9), kind=kLoop, calls=%fused_computation.5 | loop fusion | flops 4194304 | bytes 25165824 | tf_op jit(solution)/shard_map/convert_element_type | solution.py:17
  217.9 0.0 copy-done.2
  217.9 0.1 copy-done.3
  218.0 14.5 %multiply_subtract_fusion = (f32[1,8192,4,64]{3,2,1,0:T(4,128)}, f32[1,8192,4,64]{3,2,1,0:T(4,128)}) fusion(f32[1,8192,4,128]{3,2,1,0:T(4,128)S(1)} %bitcast.8, f32[8192,64]{1,0:T(8,128)S(1)} %copy-done.3, f32[8192,64]{1,0:T(8,128)S(1)} %copy-done.2), kind=kLoop, calls=%fused_computation.3 | loop fusion | flops 12582912 | bytes 37748736 | tf_op jit(solution)/shard_map/sub | solution.py:12
  232.4 0.0 copy-start
  232.4 0.0 copy-start.1
  232.4 19.4 %abs_reduce_fusion = f32[4,128]{1,0:T(4,128)S(1)} fusion(f32[1,8192,4,64]{3,2,1,0:T(4,128)} %get-tuple-element.4, f32[1,8192,4,64]{3,2,1,0:T(4,128)} %get-tuple-element.3), kind=kLoop, calls=%fused_computation.1 | loop fusion | flops 12582400 | bytes 16779264 | tf_op jit(solution)/shard_map/reduce_max | solution.py:27
  251.8 0.0 copy-done
  251.8 1.0 copy-done.1
  252.8 0.0 copy-start.4
  252.8 10.3 %divide_convert_fusion = bf16[1,8192,4,128]{3,2,1,0:T(4,128)(2,1)} fusion(f32[4,128]{1,0:T(4,128)S(1)} %abs_reduce_fusion, f32[1,8192,4,64]{3,2,1,0:T(4,128)S(1)} %copy-done.1, f32[1,8192,4,64]{3,2,1,0:T(4,128)S(1)} %copy-done), kind=kLoop, calls=%fused_computation.4 | loop fusion | flops 12582912 | bytes 25167872 | tf_op jit(solution)/shard_map/convert_element_type | solution.py:28
  263.0 0.0 copy-done.4
  263.0 119.3 %all-to-all-done.1 = bf16[16,512,4,128]{3,2,1,0:T(4,128)(2,1)} async-done(((bf16[16,512,4,128]{3,2,1,0:T(4,128)(2,1)}), bf16[16,512,4,128]{3,2,1,0:T(4,128)(2,1)}, u32[]{:S(2)}, u32[]{:S(2)}) %all-to-all-start.1) | async-done | bytes 8388640 | tf_op jit(solution)/shard_map/all_to_all | solution.py:24
  382.3 8.1 %copy.9 = bf16[1,8192,4,128]{3,2,1,0:T(4,128)(2,1)} copy(bf16[1,8192,4,128]{3,2,1,0:T(4,128)(2,1)} %bitcast.2) | data formatting | bytes 16777216
Async XLA Ops:
  189.2 193.1 %all-to-all-start.1 = ((bf16[16,512,4,128]{3,2,1,0:T(4,128)(2,1)}), bf16[16,512,4,128]{3,2,1,0:T(4,128)(2,1)}, u32[]{:S(2)}, u32[]{:S(2)}) async-start(bf16[16,512,4,128]{3,2,1,0:T(4,128)(2,1)} %param.4), calls=%async_computation.1 | async-start | bytes 16777216 | tf_op jit(solution)/shard_map/all_to_all | solution.py:24
  212.0 5.9 %copy-start.2 = (f32[8192,64]{1,0:T(8,128)S(1)}, f32[8192,64]{1,0:T(8,128)}, u32[]{:S(2)}) copy-start(f32[8192,64]{1,0:T(8,128)} %copy.6) | copy-start | bytes 6291460
  212.0 6.0 %copy-start.3 = (f32[8192,64]{1,0:T(8,128)S(1)}, f32[8192,64]{1,0:T(8,128)}, u32[]{:S(2)}) copy-start(f32[8192,64]{1,0:T(8,128)} %copy.7) | copy-start | bytes 6291460
  232.4 19.4 %copy-start = (f32[1,8192,4,64]{3,2,1,0:T(4,128)S(1)}, f32[1,8192,4,64]{3,2,1,0:T(4,128)}, u32[]{:S(2)}) copy-start(f32[1,8192,4,64]{3,2,1,0:T(4,128)} %get-tuple-element.3) | copy-start | bytes 25165828
  232.4 20.4 %copy-start.1 = (f32[1,8192,4,64]{3,2,1,0:T(4,128)S(1)}, f32[1,8192,4,64]{3,2,1,0:T(4,128)}, u32[]{:S(2)}) copy-start(f32[1,8192,4,64]{3,2,1,0:T(4,128)} %get-tuple-element.4) | copy-start | bytes 25165828
  252.8 10.3 %copy-start.4 = (f32[4,128]{1,0:T(4,128)}, f32[4,128]{1,0:T(4,128)S(1)}, u32[]{:S(2)}) copy-start(f32[4,128]{1,0:T(4,128)S(1)} %abs_reduce_fusion) | copy-start | bytes 6148
where the time goes:
time: 391 us; the launch traced here: 390 us
  blocking collectives  189 us (48%)
  waiting for transfers between devices  119 us (30%)
  other arithmetic  50 us (13%)
  local copies, waits for them, and re-layouts  25.1 us (6%)
  starting transfers between devices  6.73 us (2%)
    all_to_all x1, blocking collectives, body(): lax.all_to_all(raw_keys, ('farcp', 'nearcp'), split_axis=0, concat_axis=1...  189 us
    all_to_all x1, waiting for transfers between devices, body(): lax.all_to_all(raw_values, ('farcp', 'nearcp'), split_axis=0, concat_axis...  119 us
    reduce_max x1, other arithmetic, body(): key_scale = jnp.max(jnp.abs(turned_keys), axis=1)  19.4 us
    sub x1, other arithmetic, turn_pairs(): first * cosine - second * sine  14.5 us
    cos x2, local copies, waits for them, and re-layouts, turn_pairs(): jnp.cos(angle)[None, :, None, :]  13.3 us
    convert_element_type x1, other arithmetic, body(): narrow_keys = (turned_keys / key_scale[:, None]).astype(jnp.bfloat16)  10.3 us
    unnamed x11, local copies, waits for them, and re-layouts  9.08 us
  transfers between devices with their start and end apart: 1, of which 1 were waited for; matrix products, arithmetic and copies ran while one was open for 17% of the time, Pallas kernels for 0%

commit v1 on v0

--- a/solution.py
+++ b/solution.py
@@ -20,7 +20,15 @@
 
 def body(raw_keys, raw_values, turn_angle):
     moved_keys, stored_values = (
-        lax.all_to_all(raw_keys, ("farcp", "nearcp"), split_axis=0, concat_axis=1, tiled=True),
+        jnp.concatenate(
+            lax.all_to_all(
+                jnp.stack(jnp.split(raw_keys, lax.axis_size(("farcp", "nearcp")), axis=0)),
+                ("farcp", "nearcp"),
+                0,
+                0,
+            ),
+            axis=1,
+        ),
         lax.all_to_all(raw_values, ("farcp", "nearcp"), split_axis=0, concat_axis=1, tiled=True),
     )
     turned_keys = ready_to_store(moved_keys, turn_angle)

time: 391 us -> 412 us (1.054)
  local copies, waits for them, and re-layouts: 25.1 us -> 45.2 us
    unnamed x11 -> x26, local copies, waits for them, and re-layouts: 9.08 us -> 27.9 us
  transfers between devices with their start and end apart: 1 -> 1, of which waited for: 1 -> 1; matrix products, arithmetic and copies ran while one was open for 17% -> 16% of each run, Pallas kernels for 0% -> 0%
where the time goes in v1:
time: 412 us; the launch traced here: 410 us
  blocking collectives  188 us (46%)
  waiting for transfers between devices  119 us (29%)
  other arithmetic  50.5 us (12%)
  local copies, waits for them, and re-layouts  45.2 us (11%)
  starting transfers between devices  6.73 us (2%)
    all_to_all x1, blocking collectives, body(): lax.all_to_all(jnp.stack(jnp.split(raw_keys, lax.axis_size(('farcp', 'nea...  188 us
    all_to_all x1, waiting for transfers between devices, body(): lax.all_to_all(raw_values, ('farcp', 'nearcp'), split_axis=0, concat_axis...  119 us
    unnamed x26, local copies, waits for them, and re-layouts  27.9 us
    reduce_max x1, other arithmetic, body(): key_scale = jnp.max(jnp.abs(turned_keys), axis=1)  19.4 us
    sub x1, other arithmetic, turn_pairs(): first * cosine - second * sine  14.5 us
    cos x2, local copies, waits for them, and re-layouts, turn_pairs(): jnp.cos(angle)[None, :, None, :]  13.3 us
    convert_element_type x1, other arithmetic, body(): narrow_keys = (turned_keys / key_scale[:, None]).astype(jnp.bfloat16)  10.3 us
  transfers between devices with their start and end apart: 1, of which 1 were waited for; matrix products, arithmetic and copies ran while one was open for 16% of the time, Pallas kernels for 0%

profile of v1, /device:TPU:28, one launch (start us, length us, event | category | flops | bytes accessed | tf_op | source)
XLA Modules:
  0.0 410.3 jit_solution(16739852657971664723)
XLA Ops:
  0.6 1.2 bitcast_dynamic-update-slice_fusion.15
  1.9 1.3 bitcast_dynamic-update-slice_fusion.14
  3.1 1.3 bitcast_dynamic-update-slice_fusion.13
  4.4 1.3 bitcast_dynamic-update-slice_fusion.12
  5.6 1.3 bitcast_dynamic-update-slice_fusion.11
  6.9 1.3 bitcast_dynamic-update-slice_fusion.10
  8.2 1.3 bitcast_dynamic-update-slice_fusion.9
  9.4 1.3 bitcast_dynamic-update-slice_fusion.8
  10.7 1.3 bitcast_dynamic-update-slice_fusion.7
  12.0 1.3 bitcast_dynamic-update-slice_fusion.6
  13.2 1.3 bitcast_dynamic-update-slice_fusion.5
  14.5 1.3 bitcast_dynamic-update-slice_fusion.4
  15.7 1.3 bitcast_dynamic-update-slice_fusion.3
  17.0 1.3 bitcast_dynamic-update-slice_fusion.2
  18.3 1.3 bitcast_dynamic-update-slice_fusion.1
  19.5 1.3 bitcast_dynamic-update-slice_fusion
  20.8 188.4 %all_to_all.17 = bf16[16,1,512,4,128]{4,3,2,1,0:T(4,128)(2,1)} all-to-all(bf16[16,1,512,4,128]{4,3,2,1,0:T(4,128)(2,1)S(1)} %bitcast_dynamic-update-slice_fusion), channel_id=1, replica_groups=mesh['farcp'=4,'nearcp'=4,'tp'=2] {'farcp','nearcp'}, dimensions={0} | all-to-all | bytes 16777216 | tf_op jit(solution)/shard_map/all_to_all | solution.py:24
  209.2 6.7 %all-to-all-start.1 = ((bf16[16,512,4,128]{3,2,1,0:T(4,128)(2,1)}), bf16[16,512,4,128]{3,2,1,0:T(4,128)(2,1)}, u32[]{:S(2)}, u32[]{:S(2)}) async-start(bf16[16,512,4,128]{3,2,1,0:T(4,128)(2,1)} %param.4), calls=%async_computation.1 | async-start | bytes 16777216 | tf_op jit(solution)/shard_map/all_to_all | solution.py:32
  215.9 9.4 %fusion = (f32[8192,64]{0,1:T(8,128)}, f32[8192,64]{0,1:T(8,128)S(1)}) fusion(f32[8192,64]{0,1:T(8,128)} %param.5), kind=kLoop, calls=%fused_computation.21 | loop fusion | bytes 6291456 | tf_op jit(solution)/shard_map/cos | solution.py:9
  225.3 3.8 copy.6
  229.2 2.8 copy.7
  231.9 0.0 copy-start.2
  231.9 0.0 copy-start.3
  231.9 6.4 %convert.1 = f32[1,8192,4,128]{3,2,1,0:T(4,128)S(1)} convert(bf16[1,8192,4,128]{3,2,1,0:T(4,128)(2,1)} %bitcast.36) | non-fusion elementwise | flops 4194304 | bytes 25165824 | tf_op jit(solution)/shard_map/convert_element_type | solution.py:17
  238.3 0.0 copy-done.2
  238.3 0.0 copy-done.3
  238.4 14.5 %multiply_subtract_fusion = (f32[1,8192,4,64]{3,2,1,0:T(4,128)}, f32[1,8192,4,64]{3,2,1,0:T(4,128)}) fusion(f32[1,8192,4,128]{3,2,1,0:T(4,128)S(1)} %convert.1, f32[8192,64]{1,0:T(8,128)S(1)} %copy-done.3, f32[8192,64]{1,0:T(8,128)S(1)} %copy-done.2), kind=kLoop, calls=%fused_computation.3 | loop fusion | flops 12582912 | bytes 37748736 | tf_op jit(solution)/shard_map/sub | solution.py:12
  252.8 0.0 copy-start
  252.8 0.0 copy-start.1
  252.8 19.4 %abs_reduce_fusion = f32[4,128]{1,0:T(4,128)S(1)} fusion(f32[1,8192,4,64]{3,2,1,0:T(4,128)} %get-tuple-element.4, f32[1,8192,4,64]{3,2,1,0:T(4,128)} %get-tuple-element.3), kind=kLoop, calls=%fused_computation.1 | loop fusion | flops 12582400 | bytes 16779264 | tf_op jit(solution)/shard_map/reduce_max | solution.py:35
  272.2 0.0 copy-done
  272.2 1.0 copy-done.1
  273.2 0.0 copy-start.4
  273.2 10.3 %divide_convert_fusion = bf16[1,8192,4,128]{3,2,1,0:T(4,128)(2,1)} fusion(f32[4,128]{1,0:T(4,128)S(1)} %abs_reduce_fusion, f32[1,8192,4,64]{3,2,1,0:T(4,128)S(1)} %copy-done.1, f32[1,8192,4,64]{3,2,1,0:T(4,128)S(1)} %copy-done), kind=kLoop, calls=%fused_computation.4 | loop fusion | flops 12582912 | bytes 25167872 | tf_op jit(solution)/shard_map/convert_element_type | solution.py:36
  283.5 0.0 copy-done.4
  283.5 118.8 %all-to-all-done.1 = bf16[16,512,4,128]{3,2,1,0:T(4,128)(2,1)} async-done(((bf16[16,512,4,128]{3,2,1,0:T(4,128)(2,1)}), bf16[16,512,4,128]{3,2,1,0:T(4,128)(2,1)}, u32[]{:S(2)}, u32[]{:S(2)}) %all-to-all-start.1) | async-done | bytes 8388640 | tf_op jit(solution)/shard_map/all_to_all | solution.py:32
  402.3 8.1 %copy.24 = bf16[1,8192,4,128]{3,2,1,0:T(4,128)(2,1)} copy(bf16[1,8192,4,128]{3,2,1,0:T(4,128)(2,1)} %bitcast.18) | data formatting | bytes 16777216
Async XLA Ops:
  209.2 193.1 %all-to-all-start.1 = ((bf16[16,512,4,128]{3,2,1,0:T(4,128)(2,1)}), bf16[16,512,4,128]{3,2,1,0:T(4,128)(2,1)}, u32[]{:S(2)}, u32[]{:S(2)}) async-start(bf16[16,512,4,128]{3,2,1,0:T(4,128)(2,1)} %param.4), calls=%async_computation.1 | async-start | bytes 16777216 | tf_op jit(solution)/shard_map/all_to_all | solution.py:32
  231.9 6.4 %copy-start.2 = (f32[8192,64]{1,0:T(8,128)S(1)}, f32[8192,64]{1,0:T(8,128)}, u32[]{:S(2)}) copy-start(f32[8192,64]{1,0:T(8,128)} %copy.6) | copy-start | bytes 6291460
  231.9 6.4 %copy-start.3 = (f32[8192,64]{1,0:T(8,128)S(1)}, f32[8192,64]{1,0:T(8,128)}, u32[]{:S(2)}) copy-start(f32[8192,64]{1,0:T(8,128)} %copy.7) | copy-start | bytes 6291460
  252.8 19.4 %copy-start = (f32[1,8192,4,64]{3,2,1,0:T(4,128)S(1)}, f32[1,8192,4,64]{3,2,1,0:T(4,128)}, u32[]{:S(2)}) copy-start(f32[1,8192,4,64]{3,2,1,0:T(4,128)} %get-tuple-element.3) | copy-start | bytes 25165828
  252.8 20.4 %copy-start.1 = (f32[1,8192,4,64]{3,2,1,0:T(4,128)S(1)}, f32[1,8192,4,64]{3,2,1,0:T(4,128)}, u32[]{:S(2)}) copy-start(f32[1,8192,4,64]{3,2,1,0:T(4,128)} %get-tuple-element.4) | copy-start | bytes 25165828
  273.2 10.3 %copy-start.4 = (f32[4,128]{1,0:T(4,128)}, f32[4,128]{1,0:T(4,128)S(1)}, u32[]{:S(2)}) copy-start(f32[4,128]{1,0:T(4,128)S(1)} %abs_reduce_fusion) | copy-start | bytes 6148
